TPU v7x, 32 devices: a whole 2x2x4 slice. The times are simulated.
32 devices in a mesh: dp: 8 (over y, x, core), seq: 4 (over z).
Axes of the slice: x: 2, y: 2, z: 4, core: 2. Of those that a mesh axis runs over, the one named last changes fastest.
Arguments:
- layer_input: bfloat16 [8, 512, 2048], P('dp', 'seq'), may hold values from -6 to 6
- cotangent: bfloat16 [8, 512, 2048], P('dp', 'seq'), may hold values from -6 to 6
- ln1_gain: float32 [2048], P('dp'), may hold values from 0.5 to 1.5
- ln1_bias: float32 [2048], P('dp'), may hold values from -3 to 3
- w_qkv: bfloat16 [2048, 6144], P('dp'), may hold values from -0.125 to 0.125
- b_qkv: float32 [6144], P('dp'), may hold values from -3 to 3
- w_out: bfloat16 [2048, 2048], P('dp'), may hold values from -0.5 to 0.5
- b_out: float32 [2048], P('dp'), may hold values from -3 to 3
- ln2_gain: float32 [2048], P('dp'), may hold values from 0.5 to 1.5
- ln2_bias: float32 [2048], P('dp'), may hold values from -3 to 3
- w_up: bfloat16 [2048, 8192], P('dp'), may hold values from -0.125 to 0.125
- b_up: float32 [8192], P('dp'), may hold values from -3 to 3
- w_down: bfloat16 [8192, 2048], P('dp'), may hold values from -0.0625 to 0.0625
- b_down: float32 [2048], P('dp'), may hold values from -3 to 3
Outputs:
- output: float32 [8, 512, 2048], P('dp', 'seq')
- input_grad: float32 [8, 512, 2048], P('dp', 'seq')
- ln1_gain_grad: float32 [2048], P('dp')
- ln1_bias_grad: float32 [2048], P('dp')
- w_qkv_grad: float32 [2048, 6144], P('dp')
- b_qkv_grad: float32 [6144], P('dp')
- w_out_grad: float32 [2048, 2048], P('dp')
- b_out_grad: float32 [2048], P('dp')
- ln2_gain_grad: float32 [2048], P('dp')
- ln2_bias_grad: float32 [2048], P('dp')
- w_up_grad: float32 [2048, 8192], P('dp')
- b_up_grad: float32 [8192], P('dp')
- w_down_grad: float32 [8192, 2048], P('dp')
- b_down_grad: float32 [2048], P('dp')
All inputs are finite; a program needn't handle non-finite values.
Results may differ from a plain program's by a relative error of at most 0.029.
Values may be sent and summed in bfloat16 or wider, within the bound.
A program may use at most 640 MiB of HBM per device.

v0:
```python
import jax
import jax.numpy as jnp
from jax import lax
from jax.sharding import PartitionSpec as P

H = 8
HD = 256
ROT = 64
epsilon = 1e-05
masked_fill = -1e30


def dot(a, b, contract):
    return lax.dot_general(a, b, (contract, ((), ())), preferred_element_type=jnp.float32)


def normalize(rows):
    center = rows - jnp.mean(rows, axis=-1, keepdims=True)
    factor = lax.rsqrt(jnp.mean(center * center, axis=-1, keepdims=True) + epsilon)
    return (center * factor, factor)


def angles(positions):
    half = ROT // 2
    freqs = 10000.0 ** (-2.0 * jnp.arange(half).astype(positions.dtype) / ROT)
    theta = positions[:, None] * freqs[None, :]
    return (jnp.cos(theta), jnp.sin(theta))


def rotate(tensor, cosine, sine, direction):
    half = ROT // 2
    first_half = tensor[..., :half]
    second_half = tensor[..., half:ROT]
    return jnp.concatenate(
        [
            first_half * cosine - direction * second_half * sine,
            second_half * cosine + direction * first_half * sine,
            tensor[..., ROT:],
        ],
        axis=-1,
    )


def gather_dp(rows):
    return lax.all_gather(rows, "dp", axis=0, tiled=True)


def gather_seq(shard):
    return lax.all_gather(shard, "seq", axis=0, tiled=False)


def scatter_dp(rows):
    return lax.psum_scatter(rows, "dp", scatter_dimension=0, tiled=True)


def exchange_sum(partial, n_seq):
    slabs = partial.astype(jnp.bfloat16).reshape(n_seq, partial.shape[0] // n_seq, partial.shape[1])
    got = lax.all_to_all(slabs, "seq", split_axis=0, concat_axis=0, tiled=True)
    return jnp.sum(got.astype(jnp.float32), axis=0)


def make_local(n_dp, n_seq):

    def local(
        layer_input,
        cotangent,
        ln1_gain,
        ln1_bias,
        w_qkv,
        b_qkv,
        w_out,
        b_out,
        ln2_gain,
        ln2_bias,
        w_up,
        b_up,
        w_down,
        b_down,
    ):
        f32, bf16 = (jnp.float32, jnp.bfloat16)
        _, tok_local, width = layer_input.shape
        length = tok_local * n_seq
        own = width // n_dp
        ff = w_up.shape[1]
        ff_own = ff // n_dp
        unit = ff_own // n_seq
        heads = H // n_seq
        z = lax.axis_index("seq")
        up_own = lax.dynamic_index_in_dim(
            w_up.reshape(own, n_dp, n_seq, unit), z, 2, keepdims=False
        ).reshape(own, n_dp * unit)
        up_w = gather_dp(up_own)
        down_own = lax.dynamic_slice_in_dim(w_down, z * unit, unit, 0)
        down_w = gather_dp(down_own)
        qkv_own = lax.dynamic_slice_in_dim(
            w_qkv.reshape(own, 3, H, HD), z * heads, heads, 2
        ).reshape(own, 3 * heads * HD)
        triple_w = gather_dp(qkv_own)
        owners = n_dp // n_seq
        piece = own // n_dp
        spread = lax.all_to_all(
            w_out.reshape(n_dp, piece, width), "dp", split_axis=0, concat_axis=0, tiled=True
        )
        out_own = lax.dynamic_slice_in_dim(spread, z * owners, owners, 0)
        out_w = (
            lax.all_gather(out_own, "dp", axis=0, tiled=False)
            .transpose(1, 0, 2, 3)
            .reshape(owners * own, width)
        )
        packed = jnp.concatenate(
            [ln1_gain, ln1_bias, ln2_gain, ln2_bias, b_out, b_down, b_qkv, b_up]
        )
        gathered = lax.all_gather(packed, "dp", axis=0, tiled=False)
        gain_one, shift_one, gain_two, shift_two, out_b, down_b = (
            gathered[:, k * own : (k + 1) * own].reshape(width) for k in range(6)
        )
        base = 6 * own
        triple_b = lax.dynamic_slice_in_dim(
            gathered[:, base : base + 3 * own].reshape(3, H, HD), z * heads, heads, 1
        ).reshape(3 * heads * HD)
        up_b = lax.dynamic_index_in_dim(
            gathered[:, base + 3 * own :].reshape(n_dp, n_seq, unit), z, 1, keepdims=False
        ).reshape(n_dp * unit)
        tokens = gather_seq(layer_input.reshape(tok_local, width)).reshape(length, width)
        incoming = gather_seq(cotangent.reshape(tok_local, width)).reshape(length, width)
        normed, _ = normalize(tokens.astype(f32))
        mlp_in = (normed * gain_two + shift_two).astype(bf16)
        attn_in = (normed * gain_one + shift_one).astype(bf16)
        inner = dot(mlp_in, up_w, ((1,), (0,))) + up_b
        cumulative = 0.5 * (1.0 + lax.erf(inner * 0.7071067811865476))
        hidden = (inner * cumulative).astype(bf16)
        slope = cumulative + inner * jnp.exp(-0.5 * inner * inner) * 0.3989422804014327
        down_grad = dot(hidden, incoming, ((0,), (0,))).astype(bf16)
        inner_grad = dot(incoming, down_w, ((1,), (1,))) * slope
        inner_grad_b = inner_grad.astype(bf16)
        up_grad = dot(mlp_in, inner_grad_b, ((0,), (0,))).astype(bf16)
        mlp_out = dot(hidden, down_w, ((1,), (0,)))
        mlp_in_grad = dot(inner_grad_b, up_w, ((1,), (1,)))
        b_up_grad = jnp.sum(inner_grad, axis=0)
        ln2_gain_grad = jnp.sum(mlp_in_grad * normed, axis=0)
        ln2_bias_grad = jnp.sum(mlp_in_grad, axis=0)
        cosine, sine = angles(jnp.arange(length, dtype=jnp.int32).astype(f32))
        cosine, sine = (cosine[:, None, :], sine[:, None, :])
        triple = (dot(attn_in, triple_w, ((1,), (0,))) + triple_b).reshape(length, 3, heads, HD)
        queries = rotate(triple[:, 0], cosine, sine, 1.0).astype(bf16)
        key_rows = rotate(triple[:, 1], cosine, sine, 1.0).astype(bf16)
        values = triple[:, 2].astype(bf16)
        scores = jnp.einsum("qhd,khd->hqk", queries, key_rows, preferred_element_type=f32) * HD ** (
            -0.5
        )
        order = jnp.arange(length, dtype=jnp.int32)
        scores = jnp.where((order[None, :] <= order[:, None])[None], scores, masked_fill)
        top = jnp.max(scores, axis=-1, keepdims=True)
        logsum = top + jnp.log(jnp.sum(jnp.exp(scores - top), axis=-1, keepdims=True))
        probs_f = jnp.exp(scores - logsum)
        probs = probs_f.astype(bf16)
        context = jnp.einsum("hqk,khd->qhd", probs, values, preferred_element_type=f32).astype(bf16)
        merged = context.reshape(length, heads * HD)
        attended = dot(merged, out_w, ((1,), (0,)))
        out_grad = dot(merged, incoming, ((0,), (0,))).astype(bf16)
        context_grad = dot(incoming, out_w, ((1,), (1,))).astype(bf16).reshape(length, heads, HD)
        delta = jnp.sum(context_grad.astype(f32) * context.astype(f32), axis=-1)
        value_grad = jnp.einsum(
            "hqk,qhd->khd", probs, context_grad, preferred_element_type=f32
        ).astype(bf16)
        prob_grad = jnp.einsum("qhd,khd->hqk", context_grad, values, preferred_element_type=f32)
        score_grad = (probs_f * (prob_grad - delta.T[:, :, None]) * HD ** (-0.5)).astype(bf16)
        query_grad = jnp.einsum(
            "hqk,khd->qhd", score_grad, key_rows, preferred_element_type=f32
        ).astype(bf16)
        key_grad = jnp.einsum(
            "hqk,qhd->khd", score_grad, queries, preferred_element_type=f32
        ).astype(bf16)
        triple_grad = jnp.stack(
            [
                rotate(query_grad.astype(f32), cosine, sine, -1.0),
                rotate(key_grad.astype(f32), cosine, sine, -1.0),
                value_grad.astype(f32),
            ],
            axis=1,
        ).reshape(length, 3 * heads * HD)
        triple_grad_b = triple_grad.astype(bf16)
        b_qkv_grad = jnp.sum(triple_grad, axis=0)
        qkv_grad = dot(attn_in, triple_grad_b, ((0,), (0,))).astype(bf16)
        attn_in_grad = dot(triple_grad_b, triple_w, ((1,), (1,)))
        ln1_gain_grad = jnp.sum(attn_in_grad * normed, axis=0)
        ln1_bias_grad = jnp.sum(attn_in_grad, axis=0)
        rows = layer_input.reshape(tok_local, width).astype(f32)
        grad_rows = cotangent.reshape(tok_local, width).astype(f32)
        output = rows + (out_b + down_b) + exchange_sum(attended + mlp_out, n_seq)
        scaled = exchange_sum(attn_in_grad * gain_one + mlp_in_grad * gain_two, n_seq)
        normed_own, factor_own = normalize(rows)
        input_grad = grad_rows + factor_own * (
            scaled
            - jnp.mean(scaled, axis=-1, keepdims=True)
            - normed_own * jnp.mean(scaled * normed_own, axis=-1, keepdims=True)
        )
        down_part = gather_seq(scatter_dp(down_grad))
        down_full = down_part.reshape(ff_own, width).astype(f32)
        up_part = gather_seq(scatter_dp(up_grad))
        up_full = (
            up_part.reshape(n_seq, own, n_dp, unit)
            .transpose(1, 2, 0, 3)
            .reshape(own, ff)
            .astype(f32)
        )
        out_part = gather_seq(
            scatter_dp(
                out_grad.reshape(owners, n_dp, piece, width)
                .transpose(1, 0, 2, 3)
                .reshape(n_dp * owners * piece, width)
            )
        )
        out_full = (
            lax.all_to_all(
                out_part.reshape(n_dp, piece, width), "dp", split_axis=0, concat_axis=0, tiled=True
            )
            .reshape(own, width)
            .astype(f32)
        )
        qkv_part = gather_seq(scatter_dp(qkv_grad))
        qkv_full = (
            qkv_part.reshape(n_seq, own, 3, heads * HD)
            .transpose(1, 2, 0, 3)
            .reshape(own, 3 * width)
            .astype(f32)
        )
        here = jnp.arange(n_seq) == z
        b_up_wide = jnp.where(here[None, :, None], b_up_grad.reshape(n_dp, 1, unit), 0.0).reshape(
            n_dp, ff_own
        )
        b_qkv_wide = jnp.where(
            here[None, :, None], b_qkv_grad.reshape(3, 1, heads * HD), 0.0
        ).reshape(n_dp, 3 * own)
        b_down_grad = jnp.sum(grad_rows, axis=0)
        small = jnp.concatenate(
            [
                ln1_gain_grad.reshape(n_dp, own),
                ln1_bias_grad.reshape(n_dp, own),
                ln2_gain_grad.reshape(n_dp, own),
                ln2_bias_grad.reshape(n_dp, own),
                b_down_grad.reshape(n_dp, own),
                b_qkv_wide,
                b_up_wide,
            ],
            axis=1,
        )
        small = lax.psum(small, ("dp", "seq"))
        mine = lax.dynamic_index_in_dim(small, lax.axis_index("dp"), 0, keepdims=False)
        g1, s1, g2, s2, bd = (mine[k * own : (k + 1) * own] for k in range(5))
        bq = mine[5 * own : 8 * own]
        bu = mine[8 * own :]
        return (
            output.reshape(layer_input.shape),
            input_grad.reshape(layer_input.shape),
            g1,
            s1,
            qkv_full,
            bq,
            out_full,
            bd,
            g2,
            s2,
            up_full,
            bu,
            down_full,
            bd,
        )

    return local


def solution(mesh):
    vector, matrix, tokens = (P("dp"), P("dp", None), P("dp", "seq", None))
    in_specs = (
        tokens,
        tokens,
        vector,
        vector,
        matrix,
        vector,
        matrix,
        vector,
        vector,
        vector,
        matrix,
        vector,
        matrix,
        vector,
    )
    out_specs = (
        tokens,
        tokens,
        vector,
        vector,
        matrix,
        vector,
        matrix,
        vector,
        vector,
        vector,
        matrix,
        vector,
        matrix,
        vector,
    )
    local = make_local(mesh.shape["dp"], mesh.shape["seq"])
    return jax.shard_map(local, mesh=mesh, in_specs=in_specs, out_specs=out_specs, check_vma=False)
```

profile of v0, /device:TPU:0, one launch (start us, length us, event | category | flops | bytes accessed | tf_op | source)
XLA Modules:
  0.0 955.7 jit_solution(7400377994347457688)
XLA Ops:
  7.9 5.3 all-to-all-start
  13.3 15.4 %all-to-all-done = bf16[8,32,2048]{2,1,0:T(8,128)(2,1)} async-done(((bf16[8,32,2048]{2,1,0:T(8,128)(2,1)}), bf16[8,32,2048]{2,1,0:T(8,128)(2,1)}, u32[]{:S(2)}, u32[]{:S(2)}) %all-to-all-start) | async-done | bytes 1048608 | tf_op jit(solution)/shard_map/all_to_all | solution.py:101
  28.7 1.7 constant_dynamic-slice_fusion.3
  34.5 6.4 copy.92
  41.0 2.3 constant_dynamic-slice_fusion.2
  43.4 2.3 constant_dynamic-slice_fusion.1
  46.0 8.5 all-gather.6
  55.4 1.8 broadcast_multiply_fusion
  58.0 2.1 convert_reduce_fusion.3
  61.5 3.4 add_convert_fusion.4
  64.9 21.6 %all-gather.28.cloned.1.call-done = bf16[16,32,2048]{2,1,0:T(8,128)(2,1)} async-done(((bf16[2,32,2048]{2,1,0:T(8,128)(2,1)}), bf16[16,32,2048]{2,1,0:T(8,128)(2,1)}) %all-gather.28.cloned.1.call-update) | async-done | bytes 2097168 | tf_op jit(solution)/shard_map/all_gather | solution.py:106
  86.5 1.7 copy.91
  88.2 45.5 %all-gather.26.cloned.1.call-done = bf16[4,128,2048]{2,1,0:T(8,128)(2,1)} async-done(((bf16[1,128,2048]{2,1,0:T(8,128)(2,1)}), bf16[4,128,2048]{2,1,0:T(8,128)(2,1)}) %all-gather.26.cloned.1.call-update) | async-done | bytes 2097168 | tf_op jit(solution)/shard_map/all_gather | solution.py:49
  133.7 3.7 convolution_convert_fusion.4
  137.4 42.8 %all-gather.20.cloned.1.call-done = bf16[2048,1536]{1,0:T(8,128)(2,1)} async-done(((bf16[256,1536]{1,0:T(8,128)(2,1)}), bf16[2048,1536]{1,0:T(8,128)(2,1)}) %all-gather.20.cloned.1.call-update) | async-done | bytes 6291472 | tf_op jit(solution)/shard_map/all_gather | solution.py:45
  180.3 8.5 convolution_add_fusion
  188.8 3.9 reshape.392
  197.8 1.5 subtract_convert_fusion.1
  203.5 1.4 copy.107
  205.0 3.8 add_convert_fusion
  216.8 2.0 copy.104
  218.8 8.2 convolution_convert_fusion.2
  227.1 11.4 %all-gather.22.cloned.1.call-done = bf16[2048,2048]{0,1:T(8,128)(2,1)} async-done(((bf16[256,2048]{0,1:T(8,128)(2,1)}), bf16[2048,2048]{0,1:T(8,128)(2,1)}) %all-gather.22.cloned.1.call-update) | async-done | bytes 8388624 | tf_op jit(solution)/shard_map/all_gather | solution.py:45
  238.5 8.9 multiply_convert_fusion
  247.4 47.7 %all-gather.24.cloned.1.call-done = bf16[2048,2048]{1,0:T(8,128)(2,1)} async-done(((bf16[256,2048]{1,0:T(8,128)(2,1)}), bf16[2048,2048]{1,0:T(8,128)(2,1)}) %all-gather.24.cloned.1.call-update) | async-done | bytes 8388624 | tf_op jit(solution)/shard_map/all_gather | solution.py:45
  295.1 10.7 %fusion.43 = (f32[2048]{0:T(1024)S(1)}, bf16[512,2048]{1,0:T(8,128)(2,1)S(1)}) fusion(f32[512,2048]{1,0:T(8,128)} %get-tuple-element.92, f32[2048]{0:T(1024)S(1)} %bitcast.207, bf16[2048,2048]{1,0:T(8,128)(2,1)} %all-gather.24.cloned.1.call-done, bf16[512,2048]{1,0:T(8,128)(2,1)} %bitcast.216), kind=kOutput, calls=%fused_computation.142 | convolution fusion | flops 4307548160 | bytes 16793600 | tf_op jit(solution)/shard_map/dot_general | solution.py:14
  307.1 6.8 convolution_convert_fusion.1
  314.0 1.5 copy-done.47
  315.5 8.5 convolution_convert_fusion
  324.0 1.4 copy-done.20
  325.5 5.8 fusion.45
  331.3 10.5 %fusion.38 = (f32[2048]{0:T(1024)S(1)}, f32[2048]{0:T(1024)S(1)}, bf16[512,2048]{1,0:T(8,128)(2,1)}, f32[2048]{0:T(1024)S(1)}, f32[2048]{0:T(1024)S(1)}) fusion(f32[512]{0:T(512)S(1)} %copy-done.36, f32[512]{0:T(512)S(1)} %copy-done.34, bf16[4,128,2048]{2,1,0:T(8,128)(2,1)S(1)} %copy-done.1, f32[2048]{0:T(1024)S(1)} %bitcast.200, ...), kind=kOutput, calls=%fused_computation.137 | convolution fusion | flops 4308590592 | bytes 18927616 | tf_op jit(solution)/shard_map/dot_general | solution.py:14
  341.8 4.7 all-to-all-start.2
  346.5 7.1 fusion.44
  353.6 2.6 add_convert_fusion.2
  356.2 39.2 %all-to-all-done.2 = bf16[4,128,2048]{2,1,0:T(8,128)(2,1)} async-done(((bf16[4,128,2048]{2,1,0:T(8,128)(2,1)}), bf16[4,128,2048]{2,1,0:T(8,128)(2,1)}, u32[]{:S(2)}, u32[]{:S(2)}) %all-to-all-start.2) | async-done | bytes 2097184 | tf_op jit(solution)/shard_map/all_to_all | solution.py:58
  395.4 4.5 all-to-all-start.1
  400.5 1.5 fusion.6
  402.3 2.3 convert_reduce_fusion
  404.9 43.0 %all-to-all-done.1 = bf16[4,128,2048]{2,1,0:T(8,128)(2,1)} async-done(((bf16[4,128,2048]{2,1,0:T(8,128)(2,1)}), bf16[4,128,2048]{2,1,0:T(8,128)(2,1)}, u32[]{:S(2)}, u32[]{:S(2)}) %all-to-all-start.1) | async-done | bytes 2097184 | tf_op jit(solution)/shard_map/all_to_all | solution.py:58
  447.8 2.1 convert_reduce_fusion.2
  450.0 1.8 convert_reduce_fusion.5
  453.3 27.5 %reduce-scatter.9.cloned.1.call-done = bf16[256,2048]{1,0:T(8,128)(2,1)} async-done(((bf16[2048,2048]{1,0:T(8,128)(2,1)}), bf16[256,2048]{1,0:T(8,128)(2,1)}) %reduce-scatter.9.cloned.1.call-update) | async-done | bytes 1048592 | tf_op jit(solution)/shard_map/reduce_scatter | solution.py:53
  480.9 75.3 %reduce-scatter.11.cloned.1.call-done = bf16[256,2048]{1,0:T(8,128)(2,1)} async-done(((bf16[2048,2048]{1,0:T(8,128)(2,1)}), bf16[256,2048]{1,0:T(8,128)(2,1)}) %reduce-scatter.11.cloned.1.call-update) | async-done | bytes 1048592 | tf_op jit(solution)/shard_map/reduce_scatter | solution.py:53
  556.3 29.6 %all-gather.32.cloned.1.call-done = bf16[256,2048]{1,0:T(8,128)(2,1)} async-done(((bf16[64,2048]{1,0:T(8,128)(2,1)}), bf16[256,2048]{1,0:T(8,128)(2,1)}) %all-gather.32.cloned.1.call-update) | async-done | bytes 1048592 | tf_op jit(solution)/shard_map/all_gather | solution.py:49
  585.8 3.9 all-to-all-start.3
  589.7 15.5 %all-to-all-done.3 = bf16[8,32,2048]{2,1,0:T(8,128)(2,1)S(1)} async-done(((bf16[8,32,2048]{2,1,0:T(8,128)(2,1)}), bf16[8,32,2048]{2,1,0:T(8,128)(2,1)S(1)}, u32[]{:S(2)}, u32[]{:S(2)}) %all-to-all-start.3) | async-done | bytes 1048608 | tf_op jit(solution)/shard_map/all_to_all | solution.py:215
  605.3 1.6 bitcast_convert_fusion
  606.9 107.3 %all-reduce.2.cloned.1.call-done = f32[8,3072]{1,0:T(8,128)} async-done(((f32[8,3072]{1,0:T(8,128)}), f32[8,3072]{1,0:T(8,128)}) %all-reduce.2.cloned.1.call-update) | async-done | bytes 98320 | tf_op jit(solution)/shard_map/psum | solution.py:248
  714.2 1.4 fusion.41
  715.7 1.4 dynamic-slice.6
  717.1 1.4 dynamic-slice_reduce_fusion
  718.5 61.7 %all-gather.30.cloned.1.call-done = bf16[1024,1536]{1,0:T(8,128)(2,1)} async-done(((bf16[256,1536]{1,0:T(8,128)(2,1)}), bf16[1024,1536]{1,0:T(8,128)(2,1)}) %all-gather.30.cloned.1.call-update) | async-done | bytes 3145744 | tf_op jit(solution)/shard_map/all_gather | solution.py:49
  780.2 5.4 copy.105
  785.6 8.2 reshape.417
  793.8 6.6 copy.106
  800.4 6.6 copy.109
  806.9 54.1 %all-gather.34.cloned.1.call-done = bf16[1024,2048]{1,0:T(8,128)(2,1)} async-done(((bf16[256,2048]{1,0:T(8,128)(2,1)}), bf16[1024,2048]{1,0:T(8,128)(2,1)}) %all-gather.34.cloned.1.call-update) | async-done | bytes 4194320 | tf_op jit(solution)/shard_map/all_gather | solution.py:49
  861.0 4.3 copy.135
  865.3 4.1 bitcast_bitcast_fusion
  869.5 12.4 %copy.108 = f32[256,8,4,256]{3,2,1,0:T(4,128)} copy(f32[256,8,4,256]{3,1,0,2:T(8,128)} %bitcast_bitcast_fusion) | data formatting | bytes 16777216 | tf_op jit(solution)/shard_map/convert_element_type | solution.py:205
  881.9 10.7 %reshape.415 = f32[256,8192]{1,0:T(8,128)} reshape(f32[256,8,4,256]{3,2,1,0:T(4,128)} %copy.108) | data formatting | bytes 16777216 | tf_op jit(solution)/shard_map/convert_element_type | solution.py:205
  892.6 49.1 %all-gather.36.cloned.1.call-done = bf16[1024,2048]{1,0:T(8,128)(2,1)} async-done(((bf16[256,2048]{1,0:T(8,128)(2,1)}), bf16[1024,2048]{1,0:T(8,128)(2,1)}) %all-gather.36.cloned.1.call-update) | async-done | bytes 4194320 | tf_op jit(solution)/shard_map/all_gather | solution.py:49
  941.7 6.7 convert_element_type.310
  (215 shorter events, 29.9 us)
Async XLA Ops:
  7.2 24.1 %copy-start.12 = (bf16[256,6144]{1,0:T(8,128)(2,1)S(1)}, bf16[256,6144]{1,0:T(8,128)(2,1)}, u32[]{:S(2)}) copy-start(bf16[256,6144]{1,0:T(8,128)(2,1)} %param.18) | copy-start | bytes 9437188
  7.2 50.8 %all-gather.18.cloned.1.call-start = ((), (), s32[]{:S(2)}) async-start(), calls=%async_computation.8 | async-start | bytes 2621440 | tf_op jit(solution)/shard_map/all_gather | solution.py:49
  7.9 20.8 %all-to-all-start = ((bf16[8,32,2048]{2,1,0:T(8,128)(2,1)}), bf16[8,32,2048]{2,1,0:T(8,128)(2,1)}, u32[]{:S(2)}, u32[]{:S(2)}) async-start(bf16[8,32,2048]{2,1,0:T(8,128)(2,1)} %bitcast.187), calls=%async_computation | async-start | bytes 2097152 | tf_op jit(solution)/shard_map/all_to_all | solution.py:101
  13.3 73.2 %all-gather.28.cloned.1.call-start = ((), (), s32[]{:S(2)}) async-start(), calls=%async_computation.18 | async-start | bytes 2359296 | tf_op jit(solution)/shard_map/all_gather | solution.py:106
  30.4 103.3 %all-gather.26.cloned.1.call-start = ((), (), s32[]{:S(2)}) async-start(), calls=%async_computation.12 | async-start | bytes 2621440 | tf_op jit(solution)/shard_map/all_gather | solution.py:49
  31.2 149.1 %all-gather.20.cloned.1.call-start = ((), (), s32[]{:S(2)}) async-start(), calls=%async_computation.9 | async-start | bytes 7077888 | tf_op jit(solution)/shard_map/all_gather | solution.py:45
  34.5 204.0 %all-gather.22.cloned.1.call-start = ((), (), s32[]{:S(2)}) async-start(), calls=%async_computation.10 | async-start | bytes 9437184 | tf_op jit(solution)/shard_map/all_gather | solution.py:45
  40.9 4.9 copy-start.40
  40.9 4.9 copy-start.41
  40.9 4.9 copy-start.42
  40.9 4.9 copy-start.43
  40.9 4.9 copy-start.44
  40.9 5.0 copy-start.45
  40.9 5.0 copy-start.38
  40.9 5.0 copy-start.39
  43.3 251.8 %all-gather.24.cloned.1.call-start = ((), (), s32[]{:S(2)}) async-start(), calls=%async_computation.11 | async-start | bytes 9437184 | tf_op jit(solution)/shard_map/all_gather | solution.py:45
  45.7 356.4 %reduce-scatter.7.cloned.1.call-start = ((), (), s32[]{:S(2)}) async-start(), calls=%async_computation.15 | async-start | bytes 2359296 | tf_op jit(solution)/shard_map/reduce_scatter | solution.py:53
  58.0 2.2 copy-start
  60.1 4.8 copy-start.33
  61.5 3.4 copy-start.35
  88.2 49.2 %copy-start.6 = (bf16[2,8,32,2048]{3,2,1,0:T(8,128)(2,1)}, bf16[2,8,32,2048]{3,2,1,0:T(8,128)(2,1)S(1)}, u32[]{:S(2)}) copy-start(bf16[2,8,32,2048]{3,2,1,0:T(8,128)(2,1)S(1)} %copy.91) | copy-start | bytes 6291460
  194.6 2.2 copy-start.14
  197.8 1.6 copy-start.15
  197.8 1.6 copy-start.17
  197.8 1.6 copy-start.30
  199.3 1.6 copy-start.21
  199.3 1.6 copy-start.23
  199.4 1.6 copy-start.25
  199.4 1.6 copy-start.27
  199.4 1.6 copy-start.8
  200.6 1.6 copy-start.46
  202.1 1.4 copy-start.10
  205.0 247.6 %reduce-scatter.5.cloned.1.call-start = ((), (), s32[]{:S(2)}) async-start(), calls=%async_computation.14 | async-start | bytes 7077888 | tf_op jit(solution)/shard_map/reduce_scatter | solution.py:53
  205.0 3.8 copy-start.32
  210.0 1.2 copy-start.16
  210.0 1.3 copy-start.22
  210.0 1.5 copy-start.24
  211.5 1.2 copy-start.29
  213.2 1.3 copy-start.9
  227.0 11.5 %copy-start.19 = (bf16[512,2048]{1,0:T(8,128)(2,1)S(1)}, bf16[512,2048]{1,0:T(8,128)(2,1)}, u32[]{:S(2)}) copy-start(bf16[512,2048]{1,0:T(8,128)(2,1)} %get-tuple-element.54) | copy-start | bytes 6291460
  227.0 253.8 %reduce-scatter.9.cloned.1.call-start = ((), (), s32[]{:S(2)}) async-start(), calls=%async_computation.16 | async-start | bytes 9437184 | tf_op jit(solution)/shard_map/reduce_scatter | solution.py:53
  305.8 1.3 copy-start.49
  313.9 1.6 copy-start.47
  313.9 242.3 %reduce-scatter.11.cloned.1.call-start = ((), (), s32[]{:S(2)}) async-start(), calls=%async_computation.17 | async-start | bytes 9437184 | tf_op jit(solution)/shard_map/reduce_scatter | solution.py:53
  324.0 1.4 copy-start.20
  325.4 5.8 copy-start.1
  325.4 5.8 copy-start.34
  325.4 5.8 copy-start.36
  325.4 5.8 copy-start.50
  341.8 4.7 copy-start.48
  341.8 53.6 %all-to-all-start.2 = ((bf16[4,128,2048]{2,1,0:T(8,128)(2,1)}), bf16[4,128,2048]{2,1,0:T(8,128)(2,1)}, u32[]{:S(2)}, u32[]{:S(2)}) async-start(bf16[4,128,2048]{2,1,0:T(8,128)(2,1)} %bitcast.31), calls=%async_computation.2 | async-start | bytes 4194304 | tf_op jit(solution)/shard_map/all_to_all | solution.py:58
  346.5 7.1 copy-start.7
  346.5 7.1 copy-start.11
  356.2 43.8 %copy-start.2 = (bf16[1,128,2048]{2,1,0:T(8,128)(2,1)S(1)}, bf16[1,128,2048]{2,1,0:T(8,128)(2,1)}, u32[]{:S(2)}) copy-start(bf16[1,128,2048]{2,1,0:T(8,128)(2,1)} %param.14) | copy-start | bytes 1572868
  356.2 44.3 %copy-start.4 = (f32[512,1,2,256]{3,0,2,1:T(8,128)S(1)}, f32[512,1,2,256]{3,0,2,1:T(8,128)}, u32[]{:S(2)}) copy-start(f32[512,1,2,256]{3,0,2,1:T(8,128)} %copy-done.3) | copy-start | bytes 3145732
  395.4 52.4 %all-to-all-start.1 = ((bf16[4,128,2048]{2,1,0:T(8,128)(2,1)}), bf16[4,128,2048]{2,1,0:T(8,128)(2,1)}, u32[]{:S(2)}, u32[]{:S(2)}) async-start(bf16[4,128,2048]{2,1,0:T(8,128)(2,1)} %bitcast.15), calls=%async_computation.1 | async-start | bytes 4194304 | tf_op jit(solution)/shard_map/all_to_all | solution.py:58
  399.9 186.0 %all-gather.32.cloned.1.call-start = ((), (), s32[]{:S(2)}) async-start(), calls=%async_computation.20 | async-start | bytes 1310720 | tf_op jit(solution)/shard_map/all_gather | solution.py:49
  402.1 312.1 %all-reduce.2.cloned.1.call-start = ((), (), s32[]{:S(2)}) async-start(), calls=%async_computation.13 | async-start | bytes 196608 | tf_op jit(solution)/shard_map/psum | solution.py:248
  404.5 45.4 %copy-start.13 = (bf16[1,128,2048]{2,1,0:T(8,128)(2,1)S(1)}, bf16[1,128,2048]{2,1,0:T(8,128)(2,1)}, u32[]{:S(2)}) copy-start(bf16[1,128,2048]{2,1,0:T(8,128)(2,1)} %param.15) | copy-start | bytes 1572868
  452.5 327.7 %all-gather.30.cloned.1.call-start = ((), (), s32[]{:S(2)}) async-start(), calls=%async_computation.19 | async-start | bytes 3932160 | tf_op jit(solution)/shard_map/all_gather | solution.py:49
  453.3 407.8 %all-gather.34.cloned.1.call-start = ((), (), s32[]{:S(2)}) async-start(), calls=%async_computation.21 | async-start | bytes 5242880 | tf_op jit(solution)/shard_map/all_gather | solution.py:49
  480.9 460.8 %all-gather.36.cloned.1.call-start = ((), (), s32[]{:S(2)}) async-start(), calls=%async_computation.22 | async-start | bytes 5242880 | tf_op jit(solution)/shard_map/all_gather | solution.py:49
  585.8 19.4 %all-to-all-start.3 = ((bf16[8,32,2048]{2,1,0:T(8,128)(2,1)}), bf16[8,32,2048]{2,1,0:T(8,128)(2,1)S(1)}, u32[]{:S(2)}, u32[]{:S(2)}) async-start(bf16[8,32,2048]{2,1,0:T(8,128)(2,1)} %bitcast.188), calls=%async_computation.5 | async-start | bytes 2097152 | tf_op jit(solution)/shard_map/all_to_all | solution.py:215
  715.6 232.7 %copy-start.37 = (f32[1,256]{1,0:T(1,128)}, f32[1,256]{1,0:T(1,128)S(1)}, u32[]{:S(2)}) copy-start(f32[1,256]{1,0:T(1,128)S(1)} %get-tuple-element.77) | copy-start | bytes 3076
  (6 other events, 5.9 us)
Sparse Core Ops, SparseCore 0:
  9.6 48.3 all-gather.17
  59.9 26.5 all-gather.27
  88.1 45.6 all-gather.25
  136.1 44.1 all-gather.19
  182.6 55.8 all-gather.21
  240.8 54.2 all-gather.23
  298.4 41.1 reduce-scatter.6
  343.5 61.7 reduce-scatter.4
  409.3 71.4 reduce-scatter.8
  484.7 71.4 reduce-scatter.10
  557.8 27.9 all-gather.31
  591.3 122.9 all-reduce.1
  715.8 64.3 all-gather.29
  781.6 79.3 all-gather.33
  862.4 79.2 all-gather.35
where the time goes:
time: 961 us; the launch traced here: 956 us
  waiting for transfers between devices  690 us (72%)
  local copies, waits for them, and re-layouts  102 us (11%)
  matrix products  87.6 us (9%)
  other arithmetic  33.9 us (4%)
  starting transfers between devices  19 us (2%)
  between operations  15.1 us (2%)
    all_gather x6, waiting for transfers between devices, gather_seq(): return lax.all_gather(shard, 'seq', axis=0, tiled=False)  241 us
    psum x1, waiting for transfers between devices, local(): small = lax.psum(small, ('dp', 'seq'))  107 us
    reduce_scatter x4, waiting for transfers between devices, scatter_dp(): return lax.psum_scatter(rows, 'dp', scatter_dimension=0, tiled=True)  103 us
    all_gather x3, waiting for transfers between devices, gather_dp(): return lax.all_gather(rows, 'dp', axis=0, tiled=True)  102 us
    dot_general x12, matrix products, dot(): lax.dot_general(a, b, (contract, ((), ())), preferred_element_type=jnp.fl...  82.6 us
    all_to_all x2, waiting for transfers between devices, exchange_sum(): got = lax.all_to_all(slabs, 'seq', split_axis=0, concat_axis=0, tiled=True)  82.1 us
    unnamed x131, local copies, waits for them, and re-layouts  27.6 us
    convert_element_type x3, local copies, waits for them, and re-layouts, local(): up_full = up_part.reshape(n_seq, own, n_dp, unit).transpose(1, 2, 0, 3).r...  27.3 us
  transfers between devices with their start and end apart: 19, of which 17 were waited for; matrix products, arithmetic and copies ran while one was open for 22% of the time, Pallas kernels for 0%

commit v1 on v0

--- a/solution.py
+++ b/solution.py
@@ -245,7 +245,7 @@
             ],
             axis=1,
         )
-        small = lax.psum(small, ("dp", "seq"))
+        small = jnp.sum(jax.lax.all_gather(small, ("dp", "seq")), axis=0)
         mine = lax.dynamic_index_in_dim(small, lax.axis_index("dp"), 0, keepdims=False)
         g1, s1, g2, s2, bd = (mine[k * own : (k + 1) * own] for k in range(5))
         bq = mine[5 * own : 8 * own]

time: 961 us -> 892 us (0.928)
  waiting for transfers between devices: 690 us -> 622 us
    psum x1 -> x0, waiting for transfers between devices: 107 us -> none  [local(): small = lax.psum(small, ('dp', 'seq'))]
    all_gather x0 -> x1, waiting for transfers between devices: none -> 40.6 us  [local(): small = jnp.sum(jax.lax.all_gather(small, ('dp', 'seq')), axis=0)]
  transfers between devices with their start and end apart: 19 -> 19, of which waited for: 17 -> 17; matrix products, arithmetic and copies ran while one was open for 22% -> 23% of each run, Pallas kernels for 0% -> 0%
where the time goes in v1:
time: 892 us; the launch traced here: 887 us
  waiting for transfers between devices  622 us (70%)
  local copies, waits for them, and re-layouts  99.5 us (11%)
  matrix products  87.6 us (10%)
  other arithmetic  35.9 us (4%)
  starting transfers between devices  19 us (2%)
  between operations  15.1 us (2%)
    all_gather x6, waiting for transfers between devices, gather_seq(): return lax.all_gather(shard, 'seq', axis=0, tiled=False)  239 us
    reduce_scatter x4, waiting for transfers between devices, scatter_dp(): return lax.psum_scatter(rows, 'dp', scatter_dimension=0, tiled=True)  103 us
    all_gather x3, waiting for transfers between devices, gather_dp(): return lax.all_gather(rows, 'dp', axis=0, tiled=True)  102 us
    dot_general x12, matrix products, dot(): lax.dot_general(a, b, (contract, ((), ())), preferred_element_type=jnp.fl...  82.6 us
    all_to_all x2, waiting for transfers between devices, exchange_sum(): got = lax.all_to_all(slabs, 'seq', split_axis=0, concat_axis=0, tiled=True)  82.1 us
    all_gather x1, waiting for transfers between devices, local(): small = jnp.sum(jax.lax.all_gather(small, ('dp', 'seq')), axis=0)  40.6 us
    unnamed x131, local copies, waits for them, and re-layouts  27.6 us
    convert_element_type x3, local copies, waits for them, and re-layouts, local(): up_full = up_part.reshape(n_seq, own, n_dp, unit).transpose(1, 2, 0, 3).r...  27.3 us
  transfers between devices with their start and end apart: 19, of which 17 were waited for; matrix products, arithmetic and copies ran while one was open for 23% of the time, Pallas kernels for 0%

profile of v1, /device:TPU:0, one launch (start us, length us, event | category | flops | bytes accessed | tf_op | source)
XLA Modules:
  0.0 887.2 jit_solution(32343750500598387)
XLA Ops:
  7.9 5.3 all-to-all-start
  13.3 15.4 %all-to-all-done = bf16[8,32,2048]{2,1,0:T(8,128)(2,1)} async-done(((bf16[8,32,2048]{2,1,0:T(8,128)(2,1)}), bf16[8,32,2048]{2,1,0:T(8,128)(2,1)}, u32[]{:S(2)}, u32[]{:S(2)}) %all-to-all-start) | async-done | bytes 1048608 | tf_op jit(solution)/shard_map/all_to_all | solution.py:101
  28.7 1.7 constant_dynamic-slice_fusion.3
  33.1 1.4 reshape.390
  34.5 6.4 copy.115
  41.0 2.3 constant_dynamic-slice_fusion.2
  43.4 2.3 constant_dynamic-slice_fusion.1
  46.0 8.5 all-gather.7
  55.4 1.8 broadcast_multiply_fusion
  58.0 2.1 convert_reduce_fusion.3
  61.5 3.4 add_convert_fusion.4
  64.9 21.6 %all-gather.30.cloned.1.call-done = bf16[16,32,2048]{2,1,0:T(8,128)(2,1)} async-done(((bf16[2,32,2048]{2,1,0:T(8,128)(2,1)}), bf16[16,32,2048]{2,1,0:T(8,128)(2,1)}) %all-gather.30.cloned.1.call-update) | async-done | bytes 2097168 | tf_op jit(solution)/shard_map/all_gather | solution.py:106
  86.5 1.7 copy.114
  88.2 45.5 %all-gather.28.cloned.1.call-done = bf16[4,128,2048]{2,1,0:T(8,128)(2,1)} async-done(((bf16[1,128,2048]{2,1,0:T(8,128)(2,1)}), bf16[4,128,2048]{2,1,0:T(8,128)(2,1)}) %all-gather.28.cloned.1.call-update) | async-done | bytes 2097168 | tf_op jit(solution)/shard_map/all_gather | solution.py:49
  133.7 3.7 convolution_convert_fusion.4
  137.4 42.8 %all-gather.22.cloned.1.call-done = bf16[2048,1536]{1,0:T(8,128)(2,1)} async-done(((bf16[256,1536]{1,0:T(8,128)(2,1)}), bf16[2048,1536]{1,0:T(8,128)(2,1)}) %all-gather.22.cloned.1.call-update) | async-done | bytes 6291472 | tf_op jit(solution)/shard_map/all_gather | solution.py:45
  180.3 8.5 convolution_add_fusion
  188.8 3.9 reshape.392
  197.8 1.5 subtract_convert_fusion.1
  203.5 1.4 copy.130
  205.0 3.8 add_convert_fusion
  216.8 2.0 copy.127
  218.8 8.2 convolution_convert_fusion.2
  227.1 11.4 %all-gather.24.cloned.1.call-done = bf16[2048,2048]{0,1:T(8,128)(2,1)} async-done(((bf16[256,2048]{0,1:T(8,128)(2,1)}), bf16[2048,2048]{0,1:T(8,128)(2,1)}) %all-gather.24.cloned.1.call-update) | async-done | bytes 8388624 | tf_op jit(solution)/shard_map/all_gather | solution.py:45
  238.5 8.9 %multiply_convert_fusion = (bf16[512,2048]{1,0:T(8,128)(2,1)}, f32[512,2048]{1,0:T(8,128)}) fusion(f32[2048]{0:T(1024)S(1)} %bitcast.208, bf16[512,2048]{1,0:T(8,128)(2,1)S(1)} %copy-done.19, bf16[2048,2048]{0,1:T(8,128)(2,1)} %all-gather.24.cloned.1.call-done), kind=kOutput, calls=%fused_computation.20 | convolution fusion | flops 4301258752 | bytes 16785408 | tf_op jit(solution)/shard_map/dot_general | solution.py:14
  247.4 47.7 %all-gather.26.cloned.1.call-done = bf16[2048,2048]{1,0:T(8,128)(2,1)} async-done(((bf16[256,2048]{1,0:T(8,128)(2,1)}), bf16[2048,2048]{1,0:T(8,128)(2,1)}) %all-gather.26.cloned.1.call-update) | async-done | bytes 8388624 | tf_op jit(solution)/shard_map/all_gather | solution.py:45
  295.1 10.7 %fusion.43 = (f32[2048]{0:T(1024)S(1)}, bf16[512,2048]{1,0:T(8,128)(2,1)S(1)}) fusion(f32[512,2048]{1,0:T(8,128)} %get-tuple-element.106, f32[2048]{0:T(1024)S(1)} %bitcast.209, bf16[2048,2048]{1,0:T(8,128)(2,1)} %all-gather.26.cloned.1.call-done, bf16[512,2048]{1,0:T(8,128)(2,1)} %bitcast.218), kind=kOutput, calls=%fused_computation.143 | convolution fusion | flops 4307548160 | bytes 16793600 | tf_op jit(solution)/shard_map/dot_general | solution.py:14
  305.8 1.3 copy-done.49
  307.1 6.8 convolution_convert_fusion.1
  314.0 1.5 copy-done.47
  315.5 8.5 convolution_convert_fusion
  324.0 1.4 copy-done.20
  325.5 5.8 fusion.45
  331.3 10.5 %fusion.38 = (f32[2048]{0:T(1024)S(1)}, f32[2048]{0:T(1024)S(1)}, bf16[512,2048]{1,0:T(8,128)(2,1)}, f32[2048]{0:T(1024)S(1)}, f32[2048]{0:T(1024)S(1)}) fusion(f32[512]{0:T(512)S(1)} %copy-done.36, f32[512]{0:T(512)S(1)} %copy-done.34, bf16[4,128,2048]{2,1,0:T(8,128)(2,1)S(1)} %copy-done.1, f32[2048]{0:T(1024)S(1)} %bitcast.202, ...), kind=kOutput, calls=%fused_computation.138 | convolution fusion | flops 4308590592 | bytes 18927616 | tf_op jit(solution)/shard_map/dot_general | solution.py:14
  341.8 4.7 all-to-all-start.2
  346.5 7.1 fusion.44
  353.6 2.6 add_convert_fusion.2
  356.2 39.2 %all-to-all-done.2 = bf16[4,128,2048]{2,1,0:T(8,128)(2,1)} async-done(((bf16[4,128,2048]{2,1,0:T(8,128)(2,1)}), bf16[4,128,2048]{2,1,0:T(8,128)(2,1)}, u32[]{:S(2)}, u32[]{:S(2)}) %all-to-all-start.2) | async-done | bytes 2097184 | tf_op jit(solution)/shard_map/all_to_all | solution.py:58
  395.4 4.5 all-to-all-start.1
  400.5 1.5 fusion.6
  402.3 2.3 convert_reduce_fusion
  404.9 43.0 %all-to-all-done.1 = bf16[4,128,2048]{2,1,0:T(8,128)(2,1)} async-done(((bf16[4,128,2048]{2,1,0:T(8,128)(2,1)}), bf16[4,128,2048]{2,1,0:T(8,128)(2,1)}, u32[]{:S(2)}, u32[]{:S(2)}) %all-to-all-start.1) | async-done | bytes 2097184 | tf_op jit(solution)/shard_map/all_to_all | solution.py:58
  447.8 2.1 convert_reduce_fusion.2
  450.0 1.8 convert_reduce_fusion.5
  453.3 27.5 %reduce-scatter.9.cloned.1.call-done = bf16[256,2048]{1,0:T(8,128)(2,1)} async-done(((bf16[2048,2048]{1,0:T(8,128)(2,1)}), bf16[256,2048]{1,0:T(8,128)(2,1)}) %reduce-scatter.9.cloned.1.call-update) | async-done | bytes 1048592 | tf_op jit(solution)/shard_map/reduce_scatter | solution.py:53
  480.9 75.3 %reduce-scatter.11.cloned.1.call-done = bf16[256,2048]{1,0:T(8,128)(2,1)} async-done(((bf16[2048,2048]{1,0:T(8,128)(2,1)}), bf16[256,2048]{1,0:T(8,128)(2,1)}) %reduce-scatter.11.cloned.1.call-update) | async-done | bytes 1048592 | tf_op jit(solution)/shard_map/reduce_scatter | solution.py:53
  556.3 29.6 %all-gather.36.cloned.1.call-done = bf16[256,2048]{1,0:T(8,128)(2,1)} async-done(((bf16[64,2048]{1,0:T(8,128)(2,1)}), bf16[256,2048]{1,0:T(8,128)(2,1)}) %all-gather.36.cloned.1.call-update) | async-done | bytes 1048592 | tf_op jit(solution)/shard_map/all_gather | solution.py:49
  585.8 3.9 all-to-all-start.3
  589.7 16.0 %all-to-all-done.3 = bf16[8,32,2048]{2,1,0:T(8,128)(2,1)S(1)} async-done(((bf16[8,32,2048]{2,1,0:T(8,128)(2,1)}), bf16[8,32,2048]{2,1,0:T(8,128)(2,1)S(1)}, u32[]{:S(2)}, u32[]{:S(2)}) %all-to-all-start.3) | async-done | bytes 1048608 | tf_op jit(solution)/shard_map/all_to_all | solution.py:215
  605.8 1.6 bitcast_convert_fusion
  607.4 40.6 %all-gather.32.cloned.1.call-done = f32[256,3072]{1,0:T(8,128)} async-done(((f32[8,3072]{1,0:T(8,128)}), f32[256,3072]{1,0:T(8,128)}) %all-gather.32.cloned.1.call-update) | async-done | bytes 3145744 | tf_op jit(solution)/shard_map/all_gather | solution.py:248
  648.0 2.1 bitcast_reduce_fusion
  652.1 59.7 %all-gather.34.cloned.1.call-done = bf16[1024,1536]{1,0:T(8,128)(2,1)} async-done(((bf16[256,1536]{1,0:T(8,128)(2,1)}), bf16[1024,1536]{1,0:T(8,128)(2,1)}) %all-gather.34.cloned.1.call-update) | async-done | bytes 3145744 | tf_op jit(solution)/shard_map/all_gather | solution.py:49
  711.8 5.4 copy.128
  717.1 8.2 reshape.417
  725.3 6.6 copy.129
  731.9 6.6 copy.132
  738.5 54.1 %all-gather.38.cloned.1.call-done = bf16[1024,2048]{1,0:T(8,128)(2,1)} async-done(((bf16[256,2048]{1,0:T(8,128)(2,1)}), bf16[1024,2048]{1,0:T(8,128)(2,1)}) %all-gather.38.cloned.1.call-update) | async-done | bytes 4194320 | tf_op jit(solution)/shard_map/all_gather | solution.py:49
  792.6 4.3 copy.158
  796.9 4.1 bitcast_bitcast_fusion
  801.0 12.4 %copy.131 = f32[256,8,4,256]{3,2,1,0:T(4,128)} copy(f32[256,8,4,256]{3,1,0,2:T(8,128)} %bitcast_bitcast_fusion) | data formatting | bytes 16777216 | tf_op jit(solution)/shard_map/convert_element_type | solution.py:205
  813.4 10.7 %reshape.415 = f32[256,8192]{1,0:T(8,128)} reshape(f32[256,8,4,256]{3,2,1,0:T(4,128)} %copy.131) | data formatting | bytes 16777216 | tf_op jit(solution)/shard_map/convert_element_type | solution.py:205
  824.2 49.1 %all-gather.40.cloned.1.call-done = bf16[1024,2048]{1,0:T(8,128)(2,1)} async-done(((bf16[256,2048]{1,0:T(8,128)(2,1)}), bf16[1024,2048]{1,0:T(8,128)(2,1)}) %all-gather.40.cloned.1.call-update) | async-done | bytes 4194320 | tf_op jit(solution)/shard_map/all_gather | solution.py:49
  873.3 6.7 convert_element_type.310
  (216 shorter events, 29.2 us)
Async XLA Ops:
  7.2 24.1 %copy-start.12 = (bf16[256,6144]{1,0:T(8,128)(2,1)S(1)}, bf16[256,6144]{1,0:T(8,128)(2,1)}, u32[]{:S(2)}) copy-start(bf16[256,6144]{1,0:T(8,128)(2,1)} %param.18) | copy-start | bytes 9437188
  7.2 50.8 %all-gather.20.cloned.1.call-start = ((), (), s32[]{:S(2)}) async-start(), calls=%async_computation.8 | async-start | bytes 2621440 | tf_op jit(solution)/shard_map/all_gather | solution.py:49
  7.9 20.8 %all-to-all-start = ((bf16[8,32,2048]{2,1,0:T(8,128)(2,1)}), bf16[8,32,2048]{2,1,0:T(8,128)(2,1)}, u32[]{:S(2)}, u32[]{:S(2)}) async-start(bf16[8,32,2048]{2,1,0:T(8,128)(2,1)} %bitcast.189), calls=%async_computation | async-start | bytes 2097152 | tf_op jit(solution)/shard_map/all_to_all | solution.py:101
  13.3 73.2 %all-gather.30.cloned.1.call-start = ((), (), s32[]{:S(2)}) async-start(), calls=%async_computation.17 | async-start | bytes 2359296 | tf_op jit(solution)/shard_map/all_gather | solution.py:106
  30.4 103.3 %all-gather.28.cloned.1.call-start = ((), (), s32[]{:S(2)}) async-start(), calls=%async_computation.12 | async-start | bytes 2621440 | tf_op jit(solution)/shard_map/all_gather | solution.py:49
  31.2 149.1 %all-gather.22.cloned.1.call-start = ((), (), s32[]{:S(2)}) async-start(), calls=%async_computation.9 | async-start | bytes 7077888 | tf_op jit(solution)/shard_map/all_gather | solution.py:45
  34.5 204.0 %all-gather.24.cloned.1.call-start = ((), (), s32[]{:S(2)}) async-start(), calls=%async_computation.10 | async-start | bytes 9437184 | tf_op jit(solution)/shard_map/all_gather | solution.py:45
  40.9 4.9 copy-start.40
  40.9 4.9 copy-start.41
  40.9 4.9 copy-start.42
  40.9 4.9 copy-start.43
  40.9 4.9 copy-start.44
  40.9 5.0 copy-start.45
  40.9 5.0 copy-start.38
  40.9 5.0 copy-start.39
  43.3 251.8 %all-gather.26.cloned.1.call-start = ((), (), s32[]{:S(2)}) async-start(), calls=%async_computation.11 | async-start | bytes 9437184 | tf_op jit(solution)/shard_map/all_gather | solution.py:45
  45.7 356.4 %reduce-scatter.7.cloned.1.call-start = ((), (), s32[]{:S(2)}) async-start(), calls=%async_computation.14 | async-start | bytes 2359296 | tf_op jit(solution)/shard_map/reduce_scatter | solution.py:53
  58.0 2.2 copy-start
  60.1 4.8 copy-start.33
  61.5 3.4 copy-start.35
  88.2 49.2 %copy-start.6 = (bf16[2,8,32,2048]{3,2,1,0:T(8,128)(2,1)}, bf16[2,8,32,2048]{3,2,1,0:T(8,128)(2,1)S(1)}, u32[]{:S(2)}) copy-start(bf16[2,8,32,2048]{3,2,1,0:T(8,128)(2,1)S(1)} %copy.114) | copy-start | bytes 6291460
  194.6 2.2 copy-start.14
  197.8 1.6 copy-start.15
  197.8 1.6 copy-start.17
  197.8 1.6 copy-start.30
  199.3 1.6 copy-start.21
  199.3 1.6 copy-start.23
  199.4 1.6 copy-start.25
  199.4 1.6 copy-start.27
  199.4 1.6 copy-start.8
  200.6 1.6 copy-start.46
  202.1 1.4 copy-start.10
  205.0 247.6 %reduce-scatter.5.cloned.1.call-start = ((), (), s32[]{:S(2)}) async-start(), calls=%async_computation.13 | async-start | bytes 7077888 | tf_op jit(solution)/shard_map/reduce_scatter | solution.py:53
  205.0 3.8 copy-start.32
  210.0 1.2 copy-start.16
  210.0 1.3 copy-start.22
  210.0 1.5 copy-start.24
  211.5 1.2 copy-start.29
  213.2 1.3 copy-start.9
  227.0 11.5 %copy-start.19 = (bf16[512,2048]{1,0:T(8,128)(2,1)S(1)}, bf16[512,2048]{1,0:T(8,128)(2,1)}, u32[]{:S(2)}) copy-start(bf16[512,2048]{1,0:T(8,128)(2,1)} %get-tuple-element.68) | copy-start | bytes 6291460
  227.0 253.8 %reduce-scatter.9.cloned.1.call-start = ((), (), s32[]{:S(2)}) async-start(), calls=%async_computation.15 | async-start | bytes 9437184 | tf_op jit(solution)/shard_map/reduce_scatter | solution.py:53
  305.8 1.3 copy-start.49
  313.9 1.6 copy-start.47
  313.9 242.3 %reduce-scatter.11.cloned.1.call-start = ((), (), s32[]{:S(2)}) async-start(), calls=%async_computation.16 | async-start | bytes 9437184 | tf_op jit(solution)/shard_map/reduce_scatter | solution.py:53
  324.0 1.4 copy-start.20
  325.4 5.8 copy-start.1
  325.4 5.8 copy-start.34
  325.4 5.8 copy-start.36
  325.4 5.8 copy-start.50
  341.8 4.7 copy-start.48
  341.8 53.6 %all-to-all-start.2 = ((bf16[4,128,2048]{2,1,0:T(8,128)(2,1)}), bf16[4,128,2048]{2,1,0:T(8,128)(2,1)}, u32[]{:S(2)}, u32[]{:S(2)}) async-start(bf16[4,128,2048]{2,1,0:T(8,128)(2,1)} %bitcast.31), calls=%async_computation.2 | async-start | bytes 4194304 | tf_op jit(solution)/shard_map/all_to_all | solution.py:58
  346.5 7.1 copy-start.7
  346.5 7.1 copy-start.11
  356.2 43.8 %copy-start.2 = (bf16[1,128,2048]{2,1,0:T(8,128)(2,1)S(1)}, bf16[1,128,2048]{2,1,0:T(8,128)(2,1)}, u32[]{:S(2)}) copy-start(bf16[1,128,2048]{2,1,0:T(8,128)(2,1)} %param.14) | copy-start | bytes 1572868
  356.2 44.3 %copy-start.4 = (f32[512,1,2,256]{3,0,2,1:T(8,128)S(1)}, f32[512,1,2,256]{3,0,2,1:T(8,128)}, u32[]{:S(2)}) copy-start(f32[512,1,2,256]{3,0,2,1:T(8,128)} %copy-done.3) | copy-start | bytes 3145732
  395.4 52.4 %all-to-all-start.1 = ((bf16[4,128,2048]{2,1,0:T(8,128)(2,1)}), bf16[4,128,2048]{2,1,0:T(8,128)(2,1)}, u32[]{:S(2)}, u32[]{:S(2)}) async-start(bf16[4,128,2048]{2,1,0:T(8,128)(2,1)} %bitcast.15), calls=%async_computation.1 | async-start | bytes 4194304 | tf_op jit(solution)/shard_map/all_to_all | solution.py:58
  399.9 186.0 %all-gather.36.cloned.1.call-start = ((), (), s32[]{:S(2)}) async-start(), calls=%async_computation.20 | async-start | bytes 1310720 | tf_op jit(solution)/shard_map/all_gather | solution.py:49
  402.1 245.9 %all-gather.32.cloned.1.call-start = ((), (), s32[]{:S(2)}) async-start(), calls=%async_computation.18 | async-start | bytes 3244032 | tf_op jit(solution)/shard_map/all_gather | solution.py:248
  404.5 45.4 %copy-start.13 = (bf16[1,128,2048]{2,1,0:T(8,128)(2,1)S(1)}, bf16[1,128,2048]{2,1,0:T(8,128)(2,1)}, u32[]{:S(2)}) copy-start(bf16[1,128,2048]{2,1,0:T(8,128)(2,1)} %param.15) | copy-start | bytes 1572868
  452.5 259.2 %all-gather.34.cloned.1.call-start = ((), (), s32[]{:S(2)}) async-start(), calls=%async_computation.19 | async-start | bytes 3932160 | tf_op jit(solution)/shard_map/all_gather | solution.py:49
  453.3 339.3 %all-gather.38.cloned.1.call-start = ((), (), s32[]{:S(2)}) async-start(), calls=%async_computation.21 | async-start | bytes 5242880 | tf_op jit(solution)/shard_map/all_gather | solution.py:49
  480.9 392.4 %all-gather.40.cloned.1.call-start = ((), (), s32[]{:S(2)}) async-start(), calls=%async_computation.22 | async-start | bytes 5242880 | tf_op jit(solution)/shard_map/all_gather | solution.py:49
  585.8 19.9 %all-to-all-start.3 = ((bf16[8,32,2048]{2,1,0:T(8,128)(2,1)}), bf16[8,32,2048]{2,1,0:T(8,128)(2,1)S(1)}, u32[]{:S(2)}, u32[]{:S(2)}) async-start(bf16[8,32,2048]{2,1,0:T(8,128)(2,1)} %bitcast.190), calls=%async_computation.5 | async-start | bytes 2097152 | tf_op jit(solution)/shard_map/all_to_all | solution.py:215
  651.4 228.6 %copy-start.37 = (f32[1,256]{1,0:T(1,128)}, f32[1,256]{1,0:T(1,128)S(1)}, u32[]{:S(2)}) copy-start(f32[1,256]{1,0:T(1,128)S(1)} %get-tuple-element.91) | copy-start | bytes 3076
  (6 other events, 5.9 us)
Sparse Core Ops, SparseCore 0:
  9.6 48.3 all-gather.19
  59.9 26.5 all-gather.29
  88.1 45.6 all-gather.27
  136.1 44.1 all-gather.21
  182.6 55.8 all-gather.23
  240.8 54.2 all-gather.25
  298.4 41.1 reduce-scatter.6
  343.5 61.7 reduce-scatter.4
  409.3 71.4 reduce-scatter.8
  484.7 71.4 reduce-scatter.10
  557.8 27.9 all-gather.35
  588.6 59.3 all-gather.31
  649.6 62.1 all-gather.33
  713.2 79.3 all-gather.37
  794.0 79.2 all-gather.39
